TPU v7x, 256 devices: a whole 4x4x8 slice. The times are simulated.
256 devices in a mesh: pb: 16 (over x, y), wa: 16 (over z, core).
Axes of the slice: x: 4, y: 4, z: 8, core: 2. Of those that a mesh axis runs over, the one named last changes fastest.
Arguments:
- quartets: int32 [8192, 4, 128], P(('pb', 'wa')), may hold values from -1 to 49151, as said below
- counts: int32 [256], P(('pb', 'wa')), may hold values from 1 to 32, as said below
- eig: bfloat16 [24, 49152], P(None, 'pb'), may hold values from -1.1953125 to 1.1953125
- freq: bfloat16 [49152], P('pb'), may hold values from 0.5 to 2
- phi: bfloat16 [144, 1152], replicated, may hold values from -0.5390625 to 0.5390625
- cells: int32 [8, 9], replicated, may hold values from -2 to 2
Outputs:
- rates: float32 [49152], P(('pb', 'wa'))
Inputs may be any that keep to these rules, and one draw needn't show every extreme that they name: quartets[b, 0, n] is a mode of one of the 256 q-points of the owner group of slot b (from 0 to 3071); the other three entries are all -1 or all modes of the mesh, and then their q-points and that of the first add up as q1 + q2 = q3 + q4 on the mesh. The used slots of a device are its first counts slots; some device has exactly 32.
All inputs are finite; a program needn't handle non-finite values.
Results may differ from a plain program's by a relative error of at most 0.0023.
Values may be sent and summed in bfloat16 or wider, within the bound.
A program may use at most 64 MiB of HBM per device.

v0:
```python
import math

import jax
import jax.numpy as jnp
from jax import lax
from jax.sharding import PartitionSpec as P

QMESH = 16


smearing = 0.5


def sent_to_all(shard, axis):
    copies = jnp.broadcast_to(shard, (lax.axis_size(axis), *shard.shape))
    return lax.all_to_all(copies, axis, split_axis=0, concat_axis=0, tiled=True)


def joined_along(blocks, dim):
    lengths = list(blocks.shape[1:])
    lengths[dim] *= blocks.shape[0]
    return jnp.moveaxis(blocks, 0, dim).reshape(lengths)


def collect(shard, axis, dim):
    blocks = sent_to_all(shard, axis)
    return joined_along(blocks, dim)


def in_blocks(shard, dim, length):
    before, after = (shard.shape[:dim], shard.shape[dim + 1 :])
    return jnp.moveaxis(shard.reshape(*before, length, -1, *after), dim, 0)


def summed_on_arrival(shard, axis, dim):
    blocks = in_blocks(shard, dim, lax.axis_size(axis))
    arrived = lax.all_to_all(blocks, axis, split_axis=0, concat_axis=0, tiled=True)
    return arrived.sum(axis=0)


def outer_pair(first, second, branches):
    count = first.shape[1]
    first_re = first[:branches][:, None, :]
    first_im = first[branches:][:, None, :]
    second_re = second[:branches][None, :, :]
    second_im = second[branches:][None, :, :]
    real = (first_re * second_re - first_im * second_im).reshape(branches * branches, count)
    imag = (first_re * second_im + first_im * second_re).reshape(branches * branches, count)
    return (real, imag)


def cluster_phase(other_modes, cells, branches):
    points = other_modes // branches
    coords = [points // (QMESH * QMESH), points // QMESH % QMESH, points % QMESH]
    shift = jnp.zeros((cells.shape[0], other_modes.shape[1]), jnp.int32)
    for which in range(3):
        sign = 1 if which == 0 else -1
        for axis_c in range(3):
            shift = (
                shift
                + sign * cells[:, 3 * which + axis_c][:, None] * coords[axis_c][which][None, :]
            )
    angle = jnp.remainder(shift, QMESH).astype(jnp.float32) * (2.0 * math.pi / QMESH)
    return (jnp.cos(angle), jnp.sin(angle))


def occupation(value):
    return 1.0 / (jnp.exp(value) - 1.0)


def contributions(
    first_modes,
    other_modes,
    other_spots,
    valid,
    first_vectors,
    first_freqs,
    vectors,
    frequencies,
    phi,
    cells,
):
    branches = vectors.shape[0] // 2
    count = first_modes.shape[0]
    clusters = cells.shape[0]
    first_vec = jnp.take(first_vectors, first_modes, axis=1).astype(jnp.float32)
    first_freq = jnp.take(first_freqs, first_modes).astype(jnp.float32)
    flat_spots = other_spots.reshape(3 * count)
    gathered = jnp.take(vectors, flat_spots, axis=1).astype(jnp.float32)
    other_freq = jnp.take(frequencies, flat_spots).astype(jnp.float32).reshape(3, count)
    second_vec = gathered[:, :count]
    third_vec = gathered[:, count : 2 * count]
    fourth_vec = gathered[:, 2 * count :]
    far_re, far_im = outer_pair(third_vec, fourth_vec, branches)
    far_im = -far_im
    cosine, sine = cluster_phase(other_modes, cells, branches)
    wide_re = cosine[:, None, :] * far_re[None] - sine[:, None, :] * far_im[None]
    wide_im = cosine[:, None, :] * far_im[None] + sine[:, None, :] * far_re[None]
    wide_re = wide_re.reshape(clusters * branches * branches, count).astype(jnp.bfloat16)
    wide_im = wide_im.reshape(clusters * branches * branches, count).astype(jnp.bfloat16)
    weighted_re = jnp.dot(phi, wide_re, preferred_element_type=jnp.float32)
    weighted_im = jnp.dot(phi, wide_im, preferred_element_type=jnp.float32)
    near_re, near_im = outer_pair(first_vec, second_vec, branches)
    value_re = jnp.sum(near_re * weighted_re - near_im * weighted_im, axis=0)
    value_im = jnp.sum(near_re * weighted_im + near_im * weighted_re, axis=0)
    mismatch = first_freq + other_freq[0] - other_freq[1] - other_freq[2]
    delta = jnp.exp(-((mismatch / smearing) ** 2)) / (smearing * math.sqrt(math.pi))
    weight = (
        (1.0 + occupation(other_freq[0]))
        * occupation(other_freq[1])
        * occupation(other_freq[2])
        / occupation(first_freq)
    )
    product = first_freq * other_freq[0] * other_freq[1] * other_freq[2]
    return jnp.where(
        valid, (value_re * value_re + value_im * value_im) * delta * weight / product, 0.0
    )


def body(quartets, counts, eig, freq, phi, cells):
    local_modes = eig.shape[1]
    held = quartets.shape[0]
    block = quartets.shape[2]
    group = math.gcd(held, 16)
    table, freq_table = (collect(eig, "pb", 1), collect(freq, "pb", 0))
    total = counts[0]

    def fetch(start):
        return lax.dynamic_slice_in_dim(quartets, start, group, 0)

    rounds = (total + group - 1) // group

    def one_round(step, partial_value):
        start = (step * group).astype(jnp.int32)
        blocks = fetch(start)
        live = start + jnp.arange(group, dtype=jnp.int32) < total
        first_modes = blocks[:, 0, :].reshape(group * block)
        others = jnp.transpose(blocks[:, 1:, :], (1, 0, 2)).reshape(3, group * block)
        valid = (others[0] >= 0) & jnp.repeat(live, block)
        clamped = jnp.maximum(others, 0)
        terms = contributions(
            first_modes, clamped, clamped, valid, eig, freq, table, freq_table, phi, cells
        )
        return partial_value.at[first_modes].add(terms)

    partial_value = lax.fori_loop(0, rounds, one_round, jnp.zeros((local_modes,), jnp.float32))
    return summed_on_arrival(partial_value, "wa", 0)


def solution(mesh):
    placed = (P(("pb", "wa"), None, None), P(("pb", "wa")), P(None, "pb"), P("pb"), P(), P())
    return jax.shard_map(
        body, mesh=mesh, in_specs=placed, out_specs=P(("pb", "wa")), check_vma=False
    )
```

profile of v0, /device:TPU:1, one launch (start us, length us, event | category | flops | bytes accessed | tf_op | source)
XLA Modules:
  0.0 344.0 jit_solution(9629413055918201647)
XLA Ops:
  2.6 14.1 %all_to_all.20 = bf16[16,2,1536]{2,1,0:T(2,128)(2,1)S(1)} all-to-all(bf16[16,2,1536]{2,1,0:T(2,128)(2,1)S(1)} %reshape.931), channel_id=1, replica_groups=mesh['pb'=16,'wa'=16] {'pb'}, dimensions={0} | all-to-all | bytes 196608 | tf_op jit(solution)/shard_map/all_to_all | solution.py:16
  16.6 2.6 broadcast_in_dim.96
  19.3 3.9 %all-to-all-start = ((bf16[16,24,3072]{2,1,0:T(8,128)(2,1)}), bf16[16,24,3072]{2,1,0:T(8,128)(2,1)S(1)}, u32[]{:S(2)}, u32[]{:S(2)}) async-start(bf16[16,24,3072]{2,1,0:T(8,128)(2,1)} %broadcast_in_dim.96), calls=%async_computation | async-start | bytes 4718592 | tf_op jit(solution)/shard_map/all_to_all | solution.py:16
  26.3 25.1 %all-to-all-done = bf16[16,24,3072]{2,1,0:T(8,128)(2,1)S(1)} async-done(((bf16[16,24,3072]{2,1,0:T(8,128)(2,1)}), bf16[16,24,3072]{2,1,0:T(8,128)(2,1)S(1)}, u32[]{:S(2)}, u32[]{:S(2)}) %all-to-all-start) | async-done | bytes 2359328 | tf_op jit(solution)/shard_map/all_to_all | solution.py:16
  51.5 8.2 %copy.81 = bf16[24,16,3072]{0,2,1:T(8,128)(2,1)} copy(bf16[24,16,3072]{2,0,1:T(8,128)(2,1)S(1)} %bitcast.151) | data formatting | bytes 4718592 | tf_op jit(solution)/shard_map/while | solution.py:146
  59.7 262.5 %while.13 = (s32[]{:T(128)}, f32[3072]{0:T(1024)S(1)}, s32[]{:T(128)}, s32[32,4,128]{2,1,0:T(4,128)}, s32[]{:T(128)}, /*index=5*/bf16[24,3072]{0,1:T(8,128)(2,1)...) while((s32[]{:T(128)}, f32[3072]{0:T(1024)S(1)}, ...), condition=%wide.region_4.5_spmd, body=%wide.region_0.4_spmd.sunk | while | flops 1385340928 | bytes 61870864 | solution.py:146
  61.7 22.7 %gather_fusion.1 = bf16[6144,24]{1,0:T(8,128)(2,1)S(1)} fusion(bf16[24,49152]{0,1:T(8,128)(2,1)} %get-tuple-element.529, s32[6144]{0:T(1024)S(1)} %broadcast_clamp_fusion.4), kind=kCustom, calls=%fused_computation.1.clone.1 | custom fusion | bytes 614400 | tf_op jit(solution)/shard_map/while/body/jit(_take)/gather | solution.py:89
  86.0 2.5 fusion.51
  88.5 1.5 copy.122
  92.3 1.4 multiply_subtract_fusion.5
  94.9 1.2 sub.190
  96.8 5.2 %subtract_convert_fusion.2 = (bf16[8,144,2048]{2,1,0:T(8,128)(2,1)S(1)}, bf16[8,144,2048]{2,1,0:T(8,128)(2,1)}) fusion(f32[144,2048]{1,0:T(8,128)S(1)} %copy-done.1, f32[8,2048]{1,0:T(8,128)S(1)} %get-tuple-element.484, f32[144,2048]{1,0:T(8,128)} %sub.190, f32[8,2048]{1,0:T(8,128)S(1)} %get-tuple-element.486), kind=kLoop, calls=%fused_computation.6.clone.1 | loop fusion | flops 18874368 | bytes 11927552 | tf_op jit(solution)/shard_map/while/body/convert_element_type | solution.py:99
  101.9 2.1 convolution_bitcast_fusion.3
  106.4 6.2 %gather_fusion.2 = bf16[2048,24]{1,0:T(8,128)(2,1)S(1)} fusion(bf16[24,3072]{0,1:T(8,128)(2,1)S(1)} %copy-done.7, s32[2048]{0:T(1024)S(1)} %broadcast_clamp_fusion.5), kind=kCustom, calls=%fused_computation.clone.1 | custom fusion | bytes 204800 | tf_op jit(solution)/shard_map/while/body/jit(_take)/gather | solution.py:86
  115.3 1.4 multiply_subtract_fusion.4
  119.7 4.4 %subtract_reduce_fusion.2 = (f32[2048]{0:T(1024)S(1)}, f32[2048]{0:T(1024)S(1)}) fusion(f32[144,2048]{1,0:T(8,128)} %add.498, f32[144,2048]{1,0:T(8,128)} %sub.189, f32[144,2048]{1,0:T(8,128)S(1)} %copy-done.2, bf16[144,1152]{1,0:T(8,128)(2,1)S(1)} %copy-done.6, bf16[1152,2048]{1,0:T(8,128)(2,1)} %bitcast.148), kind=kOutput, calls=%fused_computation.15.clone.1 | convolution fusion | flops 681832448 | bytes 8605696 | tf_op jit(solution)/shard_map/while/body/dot_general | solution.py:102
  124.1 38.2 %gather_fusion = bf16[6144]{0:T(1024)(128)(2,1)S(1)} fusion(bf16[49152]{0:T(1024)(128)(2,1)S(1)} %get-tuple-element.533, s32[6144]{0:T(1024)S(1)} %copy-done.9), kind=kCustom, calls=%fused_computation.3.clone.1 | custom fusion | bytes 49152 | tf_op jit(solution)/shard_map/while/body/jit(_take)/gather | solution.py:90
  162.4 13.1 %gather_fusion.3 = bf16[2048]{0:T(1024)(128)(2,1)S(1)} fusion(bf16[3072]{0:T(1024)(128)(2,1)S(1)} %get-tuple-element.532, s32[2048]{0:T(1024)S(1)} %copy-done.14), kind=kCustom, calls=%fused_computation.2.clone.1 | custom fusion | bytes 16384 | tf_op jit(solution)/shard_map/while/body/jit(_take)/gather | solution.py:87
  176.2 14.5 %scatter_fusion = f32[3072]{0:T(1024)S(1)} fusion(f32[3072]{0:T(1024)S(1)} %get-tuple-element.508, s32[2048]{0:T(1024)S(1)} %bitcast.154, f32[2048]{0:T(1024)S(1)} %fusion.56), kind=kCustom, calls=%fused_computation.4.clone.1 | custom fusion | flops 2048 | bytes 32768 | tf_op jit(solution)/shard_map/while/body/scatter-add | solution.py:144
  192.7 22.6 %gather_fusion.1 = bf16[6144,24]{1,0:T(8,128)(2,1)S(1)} fusion(bf16[24,49152]{0,1:T(8,128)(2,1)} %get-tuple-element.529, s32[6144]{0:T(1024)S(1)} %broadcast_clamp_fusion.4), kind=kCustom, calls=%fused_computation.1.clone.1 | custom fusion | bytes 614400 | tf_op jit(solution)/shard_map/while/body/jit(_take)/gather | solution.py:89
  217.1 2.5 fusion.51
  219.5 1.5 copy.122
  223.4 1.4 multiply_subtract_fusion.5
  227.8 5.2 %subtract_convert_fusion.2 = (bf16[8,144,2048]{2,1,0:T(8,128)(2,1)S(1)}, bf16[8,144,2048]{2,1,0:T(8,128)(2,1)}) fusion(f32[144,2048]{1,0:T(8,128)S(1)} %copy-done.1, f32[8,2048]{1,0:T(8,128)S(1)} %get-tuple-element.484, f32[144,2048]{1,0:T(8,128)} %sub.190, f32[8,2048]{1,0:T(8,128)S(1)} %get-tuple-element.486), kind=kLoop, calls=%fused_computation.6.clone.1 | loop fusion | flops 18874368 | bytes 11927552 | tf_op jit(solution)/shard_map/while/body/convert_element_type | solution.py:99
  233.0 2.1 convolution_bitcast_fusion.3
  237.5 6.2 %gather_fusion.2 = bf16[2048,24]{1,0:T(8,128)(2,1)S(1)} fusion(bf16[24,3072]{0,1:T(8,128)(2,1)S(1)} %copy-done.7, s32[2048]{0:T(1024)S(1)} %broadcast_clamp_fusion.5), kind=kCustom, calls=%fused_computation.clone.1 | custom fusion | bytes 204800 | tf_op jit(solution)/shard_map/while/body/jit(_take)/gather | solution.py:86
  246.4 1.4 multiply_subtract_fusion.4
  250.7 4.4 %subtract_reduce_fusion.2 = (f32[2048]{0:T(1024)S(1)}, f32[2048]{0:T(1024)S(1)}) fusion(f32[144,2048]{1,0:T(8,128)} %add.498, f32[144,2048]{1,0:T(8,128)} %sub.189, f32[144,2048]{1,0:T(8,128)S(1)} %copy-done.2, bf16[144,1152]{1,0:T(8,128)(2,1)S(1)} %copy-done.6, bf16[1152,2048]{1,0:T(8,128)(2,1)} %bitcast.148), kind=kOutput, calls=%fused_computation.15.clone.1 | convolution fusion | flops 681832448 | bytes 8605696 | tf_op jit(solution)/shard_map/while/body/dot_general | solution.py:102
  255.2 38.2 %gather_fusion = bf16[6144]{0:T(1024)(128)(2,1)S(1)} fusion(bf16[49152]{0:T(1024)(128)(2,1)S(1)} %get-tuple-element.533, s32[6144]{0:T(1024)S(1)} %copy-done.9), kind=kCustom, calls=%fused_computation.3.clone.1 | custom fusion | bytes 49152 | tf_op jit(solution)/shard_map/while/body/jit(_take)/gather | solution.py:90
  293.4 13.1 %gather_fusion.3 = bf16[2048]{0:T(1024)(128)(2,1)S(1)} fusion(bf16[3072]{0:T(1024)(128)(2,1)S(1)} %get-tuple-element.532, s32[2048]{0:T(1024)S(1)} %copy-done.14), kind=kCustom, calls=%fused_computation.2.clone.1 | custom fusion | bytes 16384 | tf_op jit(solution)/shard_map/while/body/jit(_take)/gather | solution.py:87
  307.3 14.7 %scatter_fusion = f32[3072]{0:T(1024)S(1)} fusion(f32[3072]{0:T(1024)S(1)} %get-tuple-element.508, s32[2048]{0:T(1024)S(1)} %bitcast.154, f32[2048]{0:T(1024)S(1)} %fusion.56), kind=kCustom, calls=%fused_computation.4.clone.1 | custom fusion | flops 2048 | bytes 32768 | tf_op jit(solution)/shard_map/while/body/scatter-add | solution.py:144
  322.2 21.1 %all_to_all.21 = f32[16,1,192]{2,1,0:T(1,128)S(1)} all-to-all(f32[16,1,192]{2,1,0:T(1,128)S(1)} %all_to_all.15), channel_id=1, replica_groups=mesh['pb'=16,'wa'=16] {'wa'}, dimensions={0} | all-to-all | bytes 24576 | tf_op jit(solution)/shard_map/all_to_all | solution.py:37
  (157 shorter events, 39.8 us)
Async XLA Ops:
  19.3 4.5 %copy-start.20 = (bf16[24,3072]{1,0:T(8,128)(2,1)S(1)}, bf16[24,3072]{1,0:T(8,128)(2,1)}, u32[]{:S(2)}) copy-start(bf16[24,3072]{1,0:T(8,128)(2,1)} %param.10) | copy-start | bytes 442372
  19.3 5.7 %copy-start.22 = (s32[8,9]{1,0:T(8,128)S(1)}, s32[8,9]{1,0:T(8,128)}, u32[]{:S(2)}) copy-start(s32[8,9]{1,0:T(8,128)} %param.13) | copy-start | bytes 868
  19.3 32.2 %all-to-all-start = ((bf16[16,24,3072]{2,1,0:T(8,128)(2,1)}), bf16[16,24,3072]{2,1,0:T(8,128)(2,1)S(1)}, u32[]{:S(2)}, u32[]{:S(2)}) async-start(bf16[16,24,3072]{2,1,0:T(8,128)(2,1)} %broadcast_in_dim.96), calls=%async_computation | async-start | bytes 4718592 | tf_op jit(solution)/shard_map/all_to_all | solution.py:16
  51.5 8.2 %copy-start = (bf16[3072]{0:T(1024)(128)(2,1)S(1)}, bf16[3072]{0:T(1024)(128)(2,1)}, u32[]{:S(2)}) copy-start(bf16[3072]{0:T(1024)(128)(2,1)} %param.11) | copy-start | bytes 18436
  61.7 22.7 %copy-start.8 = (s32[6144]{0:T(1024)}, s32[6144]{0:T(1024)S(1)}, u32[]{:S(2)}) copy-start(s32[6144]{0:T(1024)S(1)} %broadcast_clamp_fusion.4) | copy-start | bytes 73732 | tf_op jit(solution)/shard_map/while
  94.9 1.8 copy-start.1
  96.8 5.2 %copy-start.5 = (bf16[144,1152]{1,0:T(8,128)(2,1)S(1)}, bf16[144,1152]{1,0:T(8,128)(2,1)}, u32[]{:S(2)}) copy-start(bf16[144,1152]{1,0:T(8,128)(2,1)} %get-tuple-element.531) | copy-start | bytes 995332 | tf_op jit(solution)/shard_map/while
  101.9 2.1 copy-start.4
  104.0 2.4 copy-start.7
  106.4 6.9 %copy-start.11 = (s32[2048,1]{0,1:T(1,128)}, s32[2048,1]{0,1:T(1,128)S(1)}, u32[]{:S(2)}) copy-start(s32[2048,1]{0,1:T(1,128)S(1)} %get-tuple-element.446) | copy-start | bytes 24580 | tf_op jit(solution)/shard_map/while
  106.4 6.9 %copy-start.15 = (s32[16,1,128]{2,1,0:T(1,128)}, s32[16,1,128]{2,1,0:T(1,128)S(1)}, u32[]{:S(2)}) copy-start(s32[16,1,128]{2,1,0:T(1,128)S(1)} %get-tuple-element.450) | copy-start | bytes 24580 | tf_op jit(solution)/shard_map/while
  106.4 6.9 %copy-start.13 = (s32[2048]{0:T(1024)}, s32[2048]{0:T(1024)S(1)}, u32[]{:S(2)}) copy-start(s32[2048]{0:T(1024)S(1)} %broadcast_clamp_fusion.5) | copy-start | bytes 24580 | tf_op jit(solution)/shard_map/while
  117.9 1.8 copy-start.6
  119.7 4.4 %copy-start.9 = (s32[6144]{0:T(1024)S(1)}, s32[6144]{0:T(1024)}, u32[]{:S(2)}) copy-start(s32[6144]{0:T(1024)} %copy-done.8) | copy-start | bytes 73732 | tf_op jit(solution)/shard_map/while
  124.1 38.2 %copy-start.18 = (pred[3,16,128]{2,1,0:T(8,128)(4,1)S(1)}, pred[3,16,128]{2,1,0:T(8,128)(4,1)}, u32[]{:S(2)}) copy-start(pred[3,16,128]{2,1,0:T(8,128)(4,1)} %copy-done.17) | copy-start | bytes 18436 | tf_op jit(solution)/shard_map/while
  124.1 38.2 %copy-start.14 = (s32[2048]{0:T(1024)S(1)}, s32[2048]{0:T(1024)}, u32[]{:S(2)}) copy-start(s32[2048]{0:T(1024)} %copy-done.13) | copy-start | bytes 24580 | tf_op jit(solution)/shard_map/while
  162.3 13.8 %copy-start.16 = (s32[16,1,128]{2,1,0:T(1,128)S(1)}, s32[16,1,128]{2,1,0:T(1,128)}, u32[]{:S(2)}) copy-start(s32[16,1,128]{2,1,0:T(1,128)} %copy-done.15) | copy-start | bytes 24580 | tf_op jit(solution)/shard_map/while
  162.3 13.9 %copy-start.12 = (s32[2048,1]{0,1:T(1,128)S(1)}, s32[2048,1]{0,1:T(1,128)}, u32[]{:S(2)}) copy-start(s32[2048,1]{0,1:T(1,128)} %copy-done.11) | copy-start | bytes 24580 | tf_op jit(solution)/shard_map/while
  192.7 22.7 %copy-start.8 = (s32[6144]{0:T(1024)}, s32[6144]{0:T(1024)S(1)}, u32[]{:S(2)}) copy-start(s32[6144]{0:T(1024)S(1)} %broadcast_clamp_fusion.4) | copy-start | bytes 73732 | tf_op jit(solution)/shard_map/while
  226.0 1.8 copy-start.1
  227.8 5.2 %copy-start.5 = (bf16[144,1152]{1,0:T(8,128)(2,1)S(1)}, bf16[144,1152]{1,0:T(8,128)(2,1)}, u32[]{:S(2)}) copy-start(bf16[144,1152]{1,0:T(8,128)(2,1)} %get-tuple-element.531) | copy-start | bytes 995332 | tf_op jit(solution)/shard_map/while
  233.0 2.1 copy-start.4
  235.1 2.4 copy-start.7
  237.4 6.9 %copy-start.11 = (s32[2048,1]{0,1:T(1,128)}, s32[2048,1]{0,1:T(1,128)S(1)}, u32[]{:S(2)}) copy-start(s32[2048,1]{0,1:T(1,128)S(1)} %get-tuple-element.446) | copy-start | bytes 24580 | tf_op jit(solution)/shard_map/while
  237.4 6.9 %copy-start.15 = (s32[16,1,128]{2,1,0:T(1,128)}, s32[16,1,128]{2,1,0:T(1,128)S(1)}, u32[]{:S(2)}) copy-start(s32[16,1,128]{2,1,0:T(1,128)S(1)} %get-tuple-element.450) | copy-start | bytes 24580 | tf_op jit(solution)/shard_map/while
  237.4 6.9 %copy-start.13 = (s32[2048]{0:T(1024)}, s32[2048]{0:T(1024)S(1)}, u32[]{:S(2)}) copy-start(s32[2048]{0:T(1024)S(1)} %broadcast_clamp_fusion.5) | copy-start | bytes 24580 | tf_op jit(solution)/shard_map/while
  249.0 1.8 copy-start.6
  250.7 4.4 %copy-start.9 = (s32[6144]{0:T(1024)S(1)}, s32[6144]{0:T(1024)}, u32[]{:S(2)}) copy-start(s32[6144]{0:T(1024)} %copy-done.8) | copy-start | bytes 73732 | tf_op jit(solution)/shard_map/while
  255.2 38.2 %copy-start.18 = (pred[3,16,128]{2,1,0:T(8,128)(4,1)S(1)}, pred[3,16,128]{2,1,0:T(8,128)(4,1)}, u32[]{:S(2)}) copy-start(pred[3,16,128]{2,1,0:T(8,128)(4,1)} %copy-done.17) | copy-start | bytes 18436 | tf_op jit(solution)/shard_map/while
  255.2 38.2 %copy-start.14 = (s32[2048]{0:T(1024)S(1)}, s32[2048]{0:T(1024)}, u32[]{:S(2)}) copy-start(s32[2048]{0:T(1024)} %copy-done.13) | copy-start | bytes 24580 | tf_op jit(solution)/shard_map/while
  293.4 13.8 %copy-start.16 = (s32[16,1,128]{2,1,0:T(1,128)S(1)}, s32[16,1,128]{2,1,0:T(1,128)}, u32[]{:S(2)}) copy-start(s32[16,1,128]{2,1,0:T(1,128)} %copy-done.15) | copy-start | bytes 24580 | tf_op jit(solution)/shard_map/while
  293.4 13.9 %copy-start.12 = (s32[2048,1]{0,1:T(1,128)S(1)}, s32[2048,1]{0,1:T(1,128)}, u32[]{:S(2)}) copy-start(s32[2048,1]{0,1:T(1,128)} %copy-done.11) | copy-start | bytes 24580 | tf_op jit(solution)/shard_map/while
  (12 other events, 14.8 us)
where the time goes:
time: 345 us; the launch traced here: 344 us
  local copies, waits for them, and re-layouts  208 us (60%)
  other arithmetic  56.8 us (16%)
  blocking collectives  35.2 us (10%)
  waiting for transfers between devices  25.1 us (7%)
  matrix products  13 us (4%)
  starting transfers between devices  3.86 us (1%)
    gather x2, local copies, waits for them, and re-layouts, contributions(): jnp.take(frequencies, flat_spots).astype(jnp.float32).reshape(3, count)  76.4 us
    gather x2, local copies, waits for them, and re-layouts, contributions(): gathered = jnp.take(vectors, flat_spots, axis=1).astype(jnp.float32)  45.3 us
    scatter-add x2, other arithmetic, one_round(): return partial_value.at[first_modes].add(terms)  29.2 us
    gather x2, local copies, waits for them, and re-layouts, contributions(): first_freq = jnp.take(first_freqs, first_modes).astype(jnp.float32)  26.2 us
    all_to_all x1, waiting for transfers between devices, sent_to_all(): return lax.all_to_all(copies, axis, split_axis=0, concat_axis=0, tiled=True)  25.1 us
    all_to_all x1, blocking collectives, summed_on_arrival(): lax.all_to_all(blocks, axis, split_axis=0, concat_axis=0, tiled=True)  21.1 us
    all_to_all x1, blocking collectives, sent_to_all(): return lax.all_to_all(copies, axis, split_axis=0, concat_axis=0, tiled=True)  14.1 us
    gather x2, local copies, waits for them, and re-layouts, contributions(): first_vec = jnp.take(first_vectors, first_modes, axis=1).astype(jnp.float32)  12.4 us
  transfers between devices with their start and end apart: 1, of which 1 were waited for; matrix products, arithmetic and copies ran while one was open for 1% of the time, Pallas kernels for 0%

commit v1 on v0

v1 whole, which is shorter than its diff:
```python
import functools
import math

import jax
import jax.numpy as jnp
import numpy as np
from jax import lax
from jax.experimental import pallas as pl
from jax.experimental.pallas import tpu as pltpu
from jax.sharding import PartitionSpec as P

QMESH = 16
BR = 12
NB = 16
LOCAL = 3072
GROUP = 768
LANES = 128
GROUP_AT = (0, 768, 1664, 2432)
FREQ_AT = 1536
WIDTH = 3200
SMEARING = 0.5
MESH = pl.DeviceIdType.MESH
NT = (((1,), (1,)), ((), ()))


def exchange_kernel(eig, freq, quartets, counts, tab, blocks, tallies, mine, send, got, lent, got_q, got_c, local):
    pb, wa = lax.axis_index("pb"), lax.axis_index("wa")
    x, y, core = pb // 4, pb % 4, wa % 2
    ahead = 1 - 2 * core
    sibling = (pb, wa + ahead)

    def place(dx, dy):
        return lax.rem(x + dx + 4, 4) * 4 + lax.rem(y + dy + 4, 4)

    mine[...] = jnp.full((1, LANES), counts[0], jnp.int32)

    barrier = pltpu.get_barrier_semaphore()
    for step in (1, -1):
        pl.semaphore_signal(barrier, inc=1, device_id=(place(step, 0), wa), device_id_type=MESH)
        pl.semaphore_signal(barrier, inc=1, device_id=(place(0, step), wa), device_id_type=MESH)
    for k in range(1, NB):
        pl.semaphore_signal(barrier, inc=1, device_id=(pb, lax.rem(wa + k, NB)), device_id_type=MESH)

    own = [
        pltpu.make_async_copy(eig.at[:, pl.ds(0, 1536)], tab.at[pb, :, pl.ds(0, 1536)], local.at[0]),
        pltpu.make_async_copy(eig.at[:, pl.ds(1536, 1536)], tab.at[pb, :, pl.ds(1664, 1536)], local.at[1]),
        pltpu.make_async_copy(freq, tab.at[pb, :, pl.ds(FREQ_AT, LANES)], local.at[2]),
        pltpu.make_async_copy(quartets.at[:, 0], blocks.at[wa], local.at[3]),
        pltpu.make_async_copy(mine, tallies.at[wa], local.at[4]),
    ]
    for copy in own:
        copy.start()
    for copy in own:
        copy.wait()

    pl.semaphore_wait(barrier, 4 + NB - 1)

    sent = []

    def push(src, dst, sem, device):
        copy = pltpu.make_async_remote_copy(
            src_ref=src, dst_ref=dst, send_sem=send.at[len(sent)], recv_sem=sem, device_id=device, device_id_type=MESH
        )
        copy.start()
        sent.append(copy)

    def piece(part, shard):
        if part == 0:
            return tab.at[shard, :, pl.ds(pl.multiple_of(core * 2432, LANES), 768)]
        return tab.at[shard, :, pl.ds(pl.multiple_of(768 + core * 768, LANES), 896)]

    def half(part, shard):
        if part == 0:
            return piece(part, shard)
        return tab.at[shard, :, pl.ds(pl.multiple_of(768 + core * 896, LANES), 768)]

    def half_of_sibling(part, shard):
        if part == 0:
            return tab.at[shard, :, pl.ds(pl.multiple_of((1 - core) * 2432, LANES), 768)]
        return tab.at[shard, :, pl.ds(pl.multiple_of(768 + (1 - core) * 896, LANES), 768)]

    def at(part, first, second):
        return place(first, second) if part == 0 else place(second, first)

    def relay(part, shard, first, second):
        view = piece(part, shard)
        push(view, view, got.at[part, shard], (at(part, first, second), wa))

    def lend(part, shard):
        view = half(part, shard)
        push(view, view, lent.at[part, shard], sibling)

    def arrived(part, shard):
        view = piece(part, shard)
        pltpu.make_async_remote_copy(
            src_ref=view, dst_ref=view, send_sem=send.at[0], recv_sem=got.at[part, shard], device_id=sibling, device_id_type=MESH
        ).wait_recv()

    def second_both(part, shard):
        relay(part, shard, 0, ahead)
        relay(part, shard, 0, -ahead)

    for part in (0, 1):
        relay(part, pb, ahead, 0)
        relay(part, pb, -ahead, 0)
    for part in (0, 1):
        second_both(part, pb)
    for k in range(1, NB):
        peer = lax.rem(wa + k, NB)
        push(quartets.at[:, k], blocks.at[wa], got_q.at[wa], (pb, peer))
        push(mine, tallies.at[wa], got_c.at[wa], (pb, peer))

    def first_axis(part, step):
        shard = at(part, step, 0)
        arrived(part, shard)
        if step is back:
            relay(part, shard, ahead, 0)
        second_both(part, shard)
        lend(part, shard)

    def second_axis(part, row, step):
        shard = at(part, row, step)
        arrived(part, shard)
        if step is back:
            relay(part, shard, 0, ahead)
        lend(part, shard)

    back, fore = -ahead, ahead
    order = [
        (first_axis, (back,)),
        (first_axis, (fore,)),
        (second_axis, (0, back)),
        (second_axis, (0, fore)),
        (first_axis, (2,)),
        (second_axis, (back, back)),
        (second_axis, (back, fore)),
        (second_axis, (0, 2)),
        (second_axis, (fore, back)),
        (second_axis, (fore, fore)),
        (second_axis, (back, 2)),
        (second_axis, (2, back)),
        (second_axis, (2, fore)),
        (second_axis, (fore, 2)),
        (second_axis, (2, 2)),
    ]
    for what, where in order:
        for part in (0, 1):
            what(part, *where)

    for k in range(1, NB):
        peer = lax.rem(wa + k, NB)
        for dst, sem in ((blocks.at[peer], got_q.at[peer]), (tallies.at[peer], got_c.at[peer])):
            pltpu.make_async_remote_copy(
                src_ref=dst, dst_ref=dst, send_sem=send.at[0], recv_sem=sem, device_id=sibling, device_id_type=MESH
            ).wait_recv()
    for part in (0, 1):
        for k in range(1, NB):
            shard = lax.rem(pb + k, NB)
            view = half_of_sibling(part, shard)
            pltpu.make_async_remote_copy(
                src_ref=view, dst_ref=view, send_sem=send.at[0], recv_sem=lent.at[part, shard], device_id=sibling, device_id_type=MESH
            ).wait_recv()
    for copy in sent:
        copy.wait_send()


def exchange(eig, freq, quartets, counts):
    any_space = pl.BlockSpec(memory_space=pl.ANY)
    vmem = pl.BlockSpec(memory_space=pltpu.VMEM)
    return pl.pallas_call(
        exchange_kernel,
        out_shape=(
            pltpu.VMEM((NB, 24, WIDTH), jnp.bfloat16),
            pltpu.VMEM((NB, 2, 4, LANES), jnp.int32),
            pltpu.VMEM((NB, 1, LANES), jnp.int32),
        ),
        in_specs=[any_space, any_space, any_space, pl.BlockSpec(memory_space=pltpu.SMEM)],
        out_specs=(vmem, vmem, vmem),
        scratch_shapes=[
            pltpu.VMEM((1, LANES), jnp.int32),
            pltpu.SemaphoreType.DMA((120,)),
            pltpu.SemaphoreType.DMA((2, NB)),
            pltpu.SemaphoreType.DMA((2, NB)),
            pltpu.SemaphoreType.DMA((NB,)),
            pltpu.SemaphoreType.DMA((NB,)),
            pltpu.SemaphoreType.DMA((5,)),
        ],
        compiler_params=pltpu.CompilerParams(collective_id=0, has_side_effects=True, vmem_limit_bytes=8 << 20),
        name="exchange",
    )(eig, freq, quartets, counts)


def selection(rows, columns, hit):
    r, c = np.meshgrid(np.arange(rows), np.arange(columns), indexing="ij")
    return jnp.asarray(hit(r, c), jnp.bfloat16)


def spread_hit(r, c):
    kind, t = r // 144, r % 144
    phonon = np.array([2, 3, 0, 1])[kind]
    component = np.where(kind % 2 == 0, t // BR, t % BR)
    return c == phonon * 16 + component


def order_hit(r, c):
    group, t = r // 32, r % 32
    lane = np.where(t < 12, t, np.where(t == 12, 24, np.where((t >= 16) & (t < 28), t - 4, -999)))
    return c == group * 32 + lane


def cosine_of(step):
    near = jnp.minimum(step, 16 - step)
    out = jnp.full(step.shape, -1.0, jnp.float32)
    for k in range(8):
        out = jnp.where(near == k, math.cos(math.pi * k / 8) if k != 4 else 0.0, out)
    return out


def floor_div(value, by):
    return jnp.floor((value.astype(jnp.float32) + 0.5) * (1.0 / by)).astype(jnp.int32)


def quartet_kernel(
    tab, blocks, tallies, phi, cells, eye, reorder, spread, out,
    table, wide, rows_v, rows_s, tally_s, live_s, near_a, near_b, sums, sem,
):
    pb, wa = lax.axis_index("pb"), lax.axis_index("wa")

    modes = jnp.maximum(blocks[...], 0)
    first = lax.broadcasted_iota(jnp.int32, modes.shape, 2) == 0
    modes = modes + jnp.where(first, pb * LOCAL, 0)
    unit = floor_div(modes, GROUP)
    rows_v[...] = (unit >> 2) * GROUP + modes - unit * GROUP
    copy_rows = pltpu.make_async_copy(rows_v, rows_s, sem.at[0])
    copy_tally = pltpu.make_async_copy(tallies, tally_s, sem.at[1])
    copy_rows.start()
    copy_tally.start()

    def turn(shard, carry):
        freq = tab[shard, :, FREQ_AT : FREQ_AT + LANES].astype(jnp.float32)
        for j in range(3):
            stack = []
            for g in range(4):
                stack.append(tab[shard, :, GROUP_AT[g] + 256 * j : GROUP_AT[g] + 256 * (j + 1)].astype(jnp.float32))
                at = 6 * g + 2 * j
                stack.append(
                    jnp.concatenate(
                        [jnp.broadcast_to(freq[at + h : at + h + 1, :], (8, LANES)) for h in range(2)], axis=1
                    )
                )
            stack = jnp.concatenate(stack, axis=0).astype(jnp.bfloat16)
            table[pl.ds(pl.multiple_of(shard * GROUP + 256 * j, 256), 256), :] = lax.dot_general(
                eye[...], stack, NT, preferred_element_type=jnp.float32
            )
        return carry

    lax.fori_loop(0, NB, turn, 0)
    copy_tally.wait()
    copy_rows.wait()

    def note(slot, total):
        source = slot >> 1
        held = ((wa - source) & (NB - 1)) + NB * (slot & 1)
        live_s[total] = slot
        return total + (held < tally_s[source, 0, 0]).astype(jnp.int32)

    live_s[0] = 0
    total = lax.fori_loop(0, 2 * NB, note, 0)
    for k in range(3):
        live_s[total + k] = 0

    sums[...] = jnp.zeros_like(sums)
    cell = cells[...].astype(jnp.float32)

    def gather(into, index):
        slot = live_s[index]
        for n in range(LANES):
            for k in range(4):
                into[k, n : n + 1, :] = table[pl.ds(rows_s[slot >> 1, slot & 1, k, n], 1), :]

    def work(held, index):
        slot = live_s[index]
        raw = blocks[slot >> 1, slot & 1]
        modes = jnp.maximum(raw, 0)
        fullmode = modes + jnp.where(lax.broadcasted_iota(jnp.int32, modes.shape, 0) == 0, pb * LOCAL, 0)
        group = floor_div(fullmode, GROUP) & 3
        halves, freqs = [], []
        for k in range(4):
            turned = lax.dot_general(reorder[...], held[k].astype(jnp.bfloat16), NT, preferred_element_type=jnp.float32)
            which = group[k : k + 1, :]
            mine = jnp.where(
                which < 2,
                jnp.where(which == 0, turned[0:32], turned[32:64]),
                jnp.where(which == 2, turned[64:96], turned[96:128]),
            )
            halves.append(jnp.concatenate([mine[0:16], mine[16:32]], axis=1))
            freqs.append(mine[12:13])
        vectors = jnp.concatenate(halves, axis=0).astype(jnp.bfloat16)
        pairs = jnp.dot(spread[...], vectors, preferred_element_type=jnp.float32)
        third, fourth, e1, e2 = (pairs[144 * k : 144 * (k + 1)] for k in range(4))
        far_re = third[:, :LANES] * fourth[:, :LANES] - third[:, LANES:] * fourth[:, LANES:]
        far_im = -(third[:, :LANES] * fourth[:, LANES:] + third[:, LANES:] * fourth[:, :LANES])

        point = floor_div(modes, BR)
        coords = [(point >> 8).astype(jnp.float32), ((point >> 4) & 15).astype(jnp.float32), (point & 15).astype(jnp.float32)]
        shift = jnp.zeros((8, LANES), jnp.float32)
        for which in range(3):
            for axis in range(3):
                column = cell[:, 3 * which + axis : 3 * which + axis + 1]
                term = column * coords[axis][which + 1 : which + 2, :]
                shift = shift + term if which == 0 else shift - term
        step = shift.astype(jnp.int32) & 15
        cosine, sine = cosine_of(step), cosine_of((step - 4) & 15)

        for k in range(8):
            c, s = cosine[k : k + 1, :], sine[k : k + 1, :]
            wide[144 * k : 144 * (k + 1), :LANES] = (c * far_re - s * far_im).astype(jnp.bfloat16)
            wide[144 * k : 144 * (k + 1), LANES:] = (c * far_im + s * far_re).astype(jnp.bfloat16)
        weighted = jnp.dot(phi[...], wide[...], preferred_element_type=jnp.float32)
        w_re, w_im = weighted[:, :LANES], weighted[:, LANES:]
        near_re = e1[:, :LANES] * e2[:, :LANES] - e1[:, LANES:] * e2[:, LANES:]
        near_im = e1[:, :LANES] * e2[:, LANES:] + e1[:, LANES:] * e2[:, :LANES]
        value_re = jnp.sum(near_re * w_re - near_im * w_im, axis=0, keepdims=True)
        value_im = jnp.sum(near_re * w_im + near_im * w_re, axis=0, keepdims=True)

        occupied = [1.0 / (jnp.exp(f) - 1.0) for f in freqs]
        mismatch = freqs[0] + freqs[1] - freqs[2] - freqs[3]
        delta = jnp.exp(-((mismatch / SMEARING) ** 2)) / (SMEARING * math.sqrt(math.pi))
        weight = (1.0 + occupied[1]) * occupied[2] * occupied[3] / occupied[0]
        product = freqs[0] * freqs[1] * freqs[2] * freqs[3]
        valid = (raw[1:2, :] >= 0) & (index < total)
        term = jnp.where(valid, (value_re * value_re + value_im * value_im) * delta * weight / product, 0.0)

        first = modes[0:1, :]
        high = floor_div(first, 192)
        low = first - 192 * high
        placed = jnp.where(lax.broadcasted_iota(jnp.int32, (NB, LANES), 0) == high, term, 0.0)
        one = placed.astype(jnp.bfloat16)
        rest = placed - one.astype(jnp.float32)
        two = rest.astype(jnp.bfloat16)
        three = (rest - two.astype(jnp.float32)).astype(jnp.bfloat16)
        spot = jnp.where(lax.broadcasted_iota(jnp.int32, (256, LANES), 0) == low, 1.0, 0.0).astype(jnp.bfloat16)
        sums[...] += lax.dot_general(
            jnp.concatenate([one, two, three], axis=0), spot, NT, preferred_element_type=jnp.float32
        )

    gather(near_a, 0)

    def two_blocks(it, carry):
        gather(near_b, 2 * it + 1)
        work(near_a, 2 * it)
        gather(near_a, 2 * it + 2)
        work(near_b, 2 * it + 1)
        return carry

    lax.fori_loop(0, (total + 1) // 2, two_blocks, 0)
    result = sums[0:16] + sums[16:32] + sums[32:48]
    for w in range(NB):
        out[w] = result[w : w + 1]


def quartet_sums(tab, blocks, tallies, phi, cells):
    vmem = pl.BlockSpec(memory_space=pltpu.VMEM)
    pinned = [pltpu.with_memory_space_constraint(a, pltpu.VMEM) for a in (tab, blocks, tallies)]
    return pl.pallas_call(
        quartet_kernel,
        out_shape=pltpu.VMEM((NB, 1, 256), jnp.float32),
        in_specs=[vmem] * 8,
        out_specs=vmem,
        scratch_shapes=[
            pltpu.VMEM((NB * GROUP, LANES), jnp.float32),
            pltpu.VMEM((1152, 256), jnp.bfloat16),
            pltpu.VMEM((NB, 2, 4, LANES), jnp.int32),
            pltpu.SMEM((NB, 2, 4, LANES), jnp.int32),
            pltpu.SMEM((NB, 1, LANES), jnp.int32),
            pltpu.SMEM((2 * NB + 4,), jnp.int32),
            pltpu.VMEM((4, LANES, LANES), jnp.float32),
            pltpu.VMEM((4, LANES, LANES), jnp.float32),
            pltpu.VMEM((48, 256), jnp.float32),
            pltpu.SemaphoreType.DMA((2,)),
        ],
        compiler_params=pltpu.CompilerParams(vmem_limit_bytes=32 << 20),
        name="quartets",
    )(
        *pinned, phi, cells,
        selection(256, 256, lambda r, c: r == c), selection(128, 128, order_hit), selection(576, 64, spread_hit),
    )


def reduce_kernel(part, out, arrived, send, recv):
    pb, wa = lax.axis_index("pb"), lax.axis_index("wa")
    barrier = pltpu.get_barrier_semaphore()
    peers = [lax.rem(wa + k, NB) for k in range(1, NB)]
    for peer in peers:
        pl.semaphore_signal(barrier, inc=1, device_id=(pb, peer), device_id_type=MESH)
    pl.semaphore_wait(barrier, NB - 1)
    sent = []
    for k, peer in enumerate(peers):
        copy = pltpu.make_async_remote_copy(
            src_ref=part.at[peer], dst_ref=arrived.at[wa], send_sem=send.at[k], recv_sem=recv.at[wa],
            device_id=(pb, peer), device_id_type=MESH,
        )
        copy.start()
        sent.append(copy)
    total = part[wa]
    for peer in peers:
        pltpu.make_async_remote_copy(
            src_ref=arrived.at[peer], dst_ref=arrived.at[peer], send_sem=send.at[0], recv_sem=recv.at[peer],
            device_id=(pb, peer), device_id_type=MESH,
        ).wait_recv()
        total = total + arrived[peer]
    out[...] = total
    for copy in sent:
        copy.wait_send()


def reduce_over_wa(part):
    vmem = pl.BlockSpec(memory_space=pltpu.VMEM)
    return pl.pallas_call(
        reduce_kernel,
        out_shape=jax.ShapeDtypeStruct((1, 256), jnp.float32),
        in_specs=[vmem],
        out_specs=vmem,
        scratch_shapes=[
            pltpu.VMEM((NB, 1, 256), jnp.float32),
            pltpu.SemaphoreType.DMA((NB,)),
            pltpu.SemaphoreType.DMA((NB,)),
        ],
        compiler_params=pltpu.CompilerParams(collective_id=1, has_side_effects=True, vmem_limit_bytes=1 << 20),
        name="reduce_wa",
    )(pltpu.with_memory_space_constraint(part, pltpu.VMEM))


def body(quartets, counts, eig, freq, phi, cells):
    dealt = quartets.reshape(2, NB, 4, LANES)
    tab, blocks, tallies = exchange(eig, freq.reshape(24, LANES), dealt, counts)
    part = quartet_sums(tab, blocks, tallies, phi, cells)
    return reduce_over_wa(part)[0, :192]


def solution(mesh):
    placed = (P(("pb", "wa"), None, None), P(("pb", "wa")), P(None, "pb"), P("pb"), P(), P())
    return jax.shard_map(body, mesh=mesh, in_specs=placed, out_specs=P(("pb", "wa")), check_vma=False)
```

time: 345 us -> 61.5 us (0.18)
  the two profiles are of different devices: /device:TPU:1 before, /device:TPU:11 now
where the time goes in v1:
time: 61.5 us; the launch traced here: 60.5 us
  Pallas kernels  52.6 us (86%)
  local copies, waits for them, and re-layouts  7.22 us (12%)
  between operations  0.7 us (1%)
    pallas_call x1, Pallas kernels, exchange(): pl.pallas_call(exchange_kernel, out_shape=(pltpu.VMEM((NB, 24, WIDTH), jn...  26.8 us
    pallas_call x1, Pallas kernels, quartet_sums(): pl.pallas_call(quartet_kernel, out_shape=pltpu.VMEM((NB, 1, 256), jnp.flo...  16.2 us
    pallas_call x1, Pallas kernels, reduce_over_wa(): pl.pallas_call(reduce_kernel, out_shape=jax.ShapeDtypeStruct((1, 256), jn...  9.56 us
    unnamed x17, local copies, waits for them, and re-layouts  7.22 us

profile of v1, /device:TPU:11, one launch (start us, length us, event | category | flops | bytes accessed | tf_op | source)
XLA Modules:
  0.0 60.5 jit_solution(2097489745863590999)
XLA Ops:
  0.7 0.0 copy-start.2
  0.7 0.9 %copy-done.2 = bf16[24,3072]{1,0:T(8,128)(2,1)S(1)} copy-done((bf16[24,3072]{1,0:T(8,128)(2,1)S(1)}, bf16[24,3072]{1,0:T(8,128)(2,1)}, u32[]{:S(2)}) %copy-start.2) | copy-done | bytes 147480
  1.6 0.0 copy-start.4
  1.6 0.8 %copy-done.4 = s32[32,4,128]{2,1,0:T(4,128)S(1)} copy-done((s32[32,4,128]{2,1,0:T(4,128)S(1)}, s32[32,4,128]{2,1,0:T(4,128)}, u32[]{:S(2)}) %copy-start.4) | copy-done | bytes 65560
  2.4 0.0 copy-start.6
  2.4 0.7 %copy-done.6 = bf16[3072]{0:T(1024)(128)(2,1)S(1)} copy-done((bf16[3072]{0:T(1024)(128)(2,1)S(1)}, bf16[3072]{0:T(1024)(128)(2,1)}, u32[]{:S(2)}) %copy-start.6) | copy-done | bytes 6168
  3.1 26.8 %exchange.1 = (bf16[16,24,3200]{2,1,0:T(8,128)(2,1)S(1)}, s32[16,2,4,128]{3,2,1,0:T(4,128)S(1)}, s32[16,1,128]{2,1,0:T(1,128)S(1)}) custom-call(bf16[24,3072]{1,0:T(8,128)(2,1)S(1)} %copy-done.2, bf16[24,128]{1,0:T(8,128)(2,1)S(1)} %bitcast.5, s32[2,16,4,128]{3,2,1,0:T(4,128)S(1)} %bitcast.4, s32[1]{0:T(128)S(6)} %copy.11.counts), custom_call_target="tpu_custom_call" | custom-call | tf_op jit(solution)/shard_map/exchange/pallas_call | solution.py:170
  29.9 0.0 copy-start
  29.9 1.0 %copy-done = bf16[144,1152]{1,0:T(8,128)(2,1)S(1)} copy-done((bf16[144,1152]{1,0:T(8,128)(2,1)S(1)}, bf16[144,1152]{1,0:T(8,128)(2,1)}, u32[]{:S(2)}) %copy-start) | copy-done | bytes 331800
  30.9 0.0 copy-start.1
  30.9 0.9 %copy-done.1 = bf16[576,64]{1,0:T(8,128)(2,1)S(1)} copy-done((bf16[576,64]{1,0:T(8,128)(2,1)S(1)}, bf16[576,64]{1,0:T(8,128)(2,1)}, u32[]{:S(2)}) %copy-start.1) | copy-done | bytes 73752
  31.8 0.0 copy-start.3
  31.8 0.9 %copy-done.3 = bf16[256,256]{1,0:T(8,128)(2,1)S(1)} copy-done((bf16[256,256]{1,0:T(8,128)(2,1)S(1)}, bf16[256,256]{1,0:T(8,128)(2,1)}, u32[]{:S(2)}) %copy-start.3) | copy-done | bytes 131096
  32.7 0.0 copy-start.5
  32.7 0.8 %copy-done.5 = bf16[128,128]{1,0:T(8,128)(2,1)S(1)} copy-done((bf16[128,128]{1,0:T(8,128)(2,1)S(1)}, bf16[128,128]{1,0:T(8,128)(2,1)}, u32[]{:S(2)}) %copy-start.5) | copy-done | bytes 32792
  33.4 0.0 copy-start.7
  33.4 0.7 %copy-done.7 = s32[8,9]{1,0:T(8,128)S(1)} copy-done((s32[8,9]{1,0:T(8,128)S(1)}, s32[8,9]{1,0:T(8,128)}, u32[]{:S(2)}) %copy-start.7) | copy-done | bytes 312
  34.1 16.2 %quartets.1.part = f32[16,1,256]{2,1,0:T(1,128)S(1)} custom-call(bf16[16,24,3200]{2,1,0:T(8,128)(2,1)S(1)} %get-tuple-element.8.tab, s32[16,2,4,128]{3,2,1,0:T(4,128)S(1)} %get-tuple-element.9.blocks, s32[16,1,128]{2,1,0:T(1,128)S(1)} %get-tuple-element.10.tallies, bf16[144,1152]{1,0:T(8,128)(2,1)S(1)} %copy-done, s32[8,9]{1,0:T(8,128)S(1)} %copy-done.7, ...), custom_call_target="tpu_custom_call" | custom-call | tf_op jit(solution)/shard_map/quartets/pallas_call | solution.py:365
  50.3 9.6 %reduce_wa.1 = f32[1,256]{1,0:T(1,128)S(1)} custom-call(f32[16,1,256]{2,1,0:T(1,128)S(1)} %quartets.1.part), custom_call_target="tpu_custom_call" | custom-call | tf_op jit(solution)/shard_map/reduce_wa/pallas_call | solution.py:419
  59.9 0.6 copy.12
Async XLA Ops:
  0.7 0.9 %copy-start.2 = (bf16[24,3072]{1,0:T(8,128)(2,1)S(1)}, bf16[24,3072]{1,0:T(8,128)(2,1)}, u32[]{:S(2)}) copy-start(bf16[24,3072]{1,0:T(8,128)(2,1)} %eig.1) | copy-start | bytes 442372
  1.6 0.8 %copy-start.4 = (s32[32,4,128]{2,1,0:T(4,128)S(1)}, s32[32,4,128]{2,1,0:T(4,128)}, u32[]{:S(2)}) copy-start(s32[32,4,128]{2,1,0:T(4,128)} %param.9) | copy-start | bytes 196612
  2.4 0.7 %copy-start.6 = (bf16[3072]{0:T(1024)(128)(2,1)S(1)}, bf16[3072]{0:T(1024)(128)(2,1)}, u32[]{:S(2)}) copy-start(bf16[3072]{0:T(1024)(128)(2,1)} %param.12) | copy-start | bytes 18436
  29.9 1.0 %copy-start = (bf16[144,1152]{1,0:T(8,128)(2,1)S(1)}, bf16[144,1152]{1,0:T(8,128)(2,1)}, u32[]{:S(2)}) copy-start(bf16[144,1152]{1,0:T(8,128)(2,1)} %phi.1) | copy-start | bytes 995332
  30.9 0.9 %copy-start.1 = (bf16[576,64]{1,0:T(8,128)(2,1)S(1)}, bf16[576,64]{1,0:T(8,128)(2,1)}, u32[]{:S(2)}) copy-start(bf16[576,64]{1,0:T(8,128)(2,1)} %constant.8.clone.spread) | copy-start | bytes 221188
  31.8 0.9 %copy-start.3 = (bf16[256,256]{1,0:T(8,128)(2,1)S(1)}, bf16[256,256]{1,0:T(8,128)(2,1)}, u32[]{:S(2)}) copy-start(bf16[256,256]{1,0:T(8,128)(2,1)} %constant.6.clone.eye) | copy-start | bytes 393220
  32.7 0.8 %copy-start.5 = (bf16[128,128]{1,0:T(8,128)(2,1)S(1)}, bf16[128,128]{1,0:T(8,128)(2,1)}, u32[]{:S(2)}) copy-start(bf16[128,128]{1,0:T(8,128)(2,1)} %constant.7.clone.reorder) | copy-start | bytes 98308
  33.4 0.7 %copy-start.7 = (s32[8,9]{1,0:T(8,128)S(1)}, s32[8,9]{1,0:T(8,128)}, u32[]{:S(2)}) copy-start(s32[8,9]{1,0:T(8,128)} %cells.1) | copy-start | bytes 868
